TPU v7x, 32 devices: a whole 2x2x4 slice. The times are simulated.
32 devices in a mesh: pipe: 2 (over y), dp: 4 (over z), tensor: 4 (over x, core).
Axes of the slice: x: 2, y: 2, z: 4, core: 2. Of those that a mesh axis runs over, the one named last changes fastest.
Arguments:
- saved: bfloat16 [2, 2, 256, 1024], P('pipe', None, 'dp'), may hold values from -6 to 6
- top_grad: bfloat16 [2, 256, 1024], P(None, 'dp'), may hold values from -6 to 6
- gain: bfloat16 [2, 1024], P('pipe', 'dp'), may hold values from 0.25 to 1.75
- w_query: bfloat16 [2, 1024, 1536], P('pipe', 'dp', 'tensor'), may hold values from -0.1875 to 0.1875
- w_latent: bfloat16 [2, 1024, 576], P('pipe', 'dp'), may hold values from -0.1875 to 0.1875
- compressed_gain: bfloat16 [2, 512], P('pipe', 'dp'), may hold values from 0.25 to 1.75
- expand_weight: bfloat16 [2, 512, 2048], P('pipe', 'dp', 'tensor'), may hold values from -0.25 to 0.25
- w_output: bfloat16 [2, 1024, 1024], P('pipe', 'tensor', 'dp'), may hold values from -0.1875 to 0.1875
Outputs:
- input_grad: bfloat16 [2, 2, 256, 1024], P('pipe', None, ('dp', 'tensor'))
- grad_gain: float32 [2, 1024], P('pipe', 'dp')
- grad_query: float32 [2, 1024, 1536], P('pipe', 'dp', 'tensor')
- grad_latent: float32 [2, 1024, 576], P('pipe', 'dp')
- grad_latent_gain: float32 [2, 512], P('pipe', 'dp')
- grad_expand: float32 [2, 512, 2048], P('pipe', 'dp', 'tensor')
- grad_output: float32 [2, 1024, 1024], P('pipe', 'tensor', 'dp')
All inputs are finite; a program needn't handle non-finite values.
Results may differ from a plain program's by a relative error of at most 0.04.
Values may be sent and summed in bfloat16 or wider, within the bound.
A program may use at most 64 MiB of HBM per device.

v0:
```python
import jax
import jax.numpy as jnp
from jax import lax
from jax.sharding import PartitionSpec as P

NOPE = 128
ROPE = 64
VDIM = 128
COMPRESSED_RANK = 512


EPS = 1e-06


def passed_along(value, axis, steps):
    count = lax.axis_size(axis)
    first, last = (max(0, -steps), min(count, count - steps))
    return lax.ppermute(value, axis, [(source, source + steps) for source in range(first, last)])


def root_mean_scale(values, scale):
    return values * lax.rsqrt(jnp.mean(values * values, axis=-1, keepdims=True) + EPS) * scale


def rotary_angles(values):
    length = values.shape[0]
    half = values.shape[-1] // 2
    freq = jnp.exp(-jnp.log(10000.0) * jnp.arange(half, dtype=jnp.float32) / half)
    angle = jnp.arange(length, dtype=jnp.float32)[:, None] * freq[None, :]
    cosine = jnp.cos(angle)[:, None, :]
    sine = jnp.sin(angle)[:, None, :]
    first = values[..., :half]
    second = values[..., half:]
    return jnp.concatenate(
        [first * cosine - second * sine, second * cosine + first * sine], axis=-1
    )


def branch(normed, w_q, w_lat, latent_norm_gain, w_exp, w_out):
    length = normed.shape[0]
    heads = w_q.shape[1] // (NOPE + ROPE)
    rounded = normed.astype(jnp.bfloat16)
    query = jnp.dot(rounded, w_q, preferred_element_type=jnp.float32).reshape(
        length, heads, NOPE + ROPE
    )
    latent_state = jnp.dot(rounded, w_lat, preferred_element_type=jnp.float32)
    compressed_state = root_mean_scale(latent_state[:, :COMPRESSED_RANK], latent_norm_gain).astype(
        jnp.bfloat16
    )
    rotary_key_part = rotary_angles(latent_state[:, None, COMPRESSED_RANK:])[:, 0, :]
    expanded = jnp.dot(compressed_state, w_exp, preferred_element_type=jnp.float32).reshape(
        length, heads, NOPE + VDIM
    )
    key_nope = expanded[:, :, :NOPE]
    values = expanded[:, :, NOPE:].astype(jnp.bfloat16)
    query_rope = rotary_angles(query[:, :, NOPE:])
    scores = jnp.einsum("qhd,khd->hqk", query[:, :, :NOPE], key_nope) + jnp.einsum(
        "qhd,kd->hqk", query_rope, rotary_key_part
    )
    scores = scores * (NOPE + ROPE) ** (-0.5)
    causal = jnp.arange(length)[:, None] >= jnp.arange(length)[None, :]
    scores = jnp.where(causal[None], scores, -1e30)
    weights = jax.nn.softmax(scores, axis=-1).astype(jnp.bfloat16)
    mixed = jnp.einsum("hqk,khd->qhd", weights.astype(jnp.float32), values.astype(jnp.float32))
    mixed = mixed.astype(jnp.bfloat16).reshape(length, heads * VDIM)
    return jnp.dot(mixed, w_out, preferred_element_type=jnp.float32)


def shards(saved, top_grad, gain, w_query, w_latent, compressed_gain, expand_weight, w_output):
    gathered = (
        lax.all_gather(gain, "dp", axis=1, tiled=True),
        lax.all_gather(w_query, "dp", axis=1, tiled=True),
        lax.all_gather(w_latent, "dp", axis=1, tiled=True),
        lax.all_gather(compressed_gain, "dp", axis=1, tiled=True),
        lax.all_gather(expand_weight, "dp", axis=1, tiled=True),
        lax.all_gather(w_output, "dp", axis=2, tiled=True),
    )
    gain32 = gathered[0][0].astype(jnp.float32)
    query_all = gathered[1][0]
    latent_all = gathered[2][0]
    lgain32 = gathered[3][0].astype(jnp.float32)
    expand_all = gathered[4][0]
    output_all = gathered[5][0]
    sections = lax.axis_size("pipe")
    section_index = lax.axis_index("pipe")
    tensor_count = lax.axis_size("tensor")
    tensor_rank = lax.axis_index("tensor")
    micro_count = saved.shape[1]
    length = saved.shape[2]
    width = saved.shape[3]
    share = length // tensor_count

    def compute(normed, upstream):
        unused, pull = jax.vjp(
            lambda value: branch(value, query_all, latent_all, lgain32, expand_all, output_all),
            normed,
        )
        return pull(upstream.astype(jnp.float32))[0]

    def skip(normed, upstream):
        return jnp.zeros_like(normed)

    gain_total = jnp.zeros((width,), jnp.float32)
    results = jnp.zeros((micro_count, share, width), jnp.bfloat16)
    stored = jnp.zeros((micro_count, length, width), jnp.bfloat16)
    received = jnp.zeros((length, width), jnp.bfloat16)
    for tick in range(sections + micro_count - 1):
        micro = tick - (sections - 1 - section_index)
        active = jnp.logical_and(micro >= 0, micro < micro_count)
        picked = jnp.clip(micro, 0, micro_count - 1)
        x_rows = lax.dynamic_index_in_dim(saved[0], picked, 0, keepdims=False)
        top_rows = lax.dynamic_index_in_dim(top_grad, picked, 0, keepdims=False)
        arrived = received
        upstream = jnp.where(section_index == sections - 1, top_rows, arrived)
        x_float = x_rows.astype(jnp.float32)
        normed, norm_pull = jax.vjp(root_mean_scale, x_float, gain32)
        branch_grad = lax.cond(active, compute, skip, normed, upstream)
        d_normed = lax.psum(branch_grad.astype(jnp.bfloat16), "tensor").astype(jnp.float32)
        dx_norm, d_gain = norm_pull(d_normed)
        dx = (upstream.astype(jnp.float32) + dx_norm).astype(jnp.bfloat16)
        gain_total = gain_total + jnp.where(active, d_gain, 0.0)
        mine = lax.dynamic_slice_in_dim(dx, tensor_rank * share, share, 0)
        chosen = (jnp.arange(micro_count) == micro)[:, None, None]
        results = jnp.where(chosen, mine[None], results)
        stored = jnp.where(chosen, upstream[None], stored)
        received = passed_along(dx, "pipe", -1)
    totals = (
        jnp.zeros(query_all.shape, jnp.float32),
        jnp.zeros(latent_all.shape, jnp.float32),
        jnp.zeros(lgain32.shape, jnp.float32),
        jnp.zeros(expand_all.shape, jnp.float32),
        jnp.zeros(output_all.shape, jnp.float32),
    )
    for micro_index in range(micro_count):
        normed_again = root_mean_scale(saved[0, micro_index].astype(jnp.float32), gain32)
        unused, weight_pull = jax.vjp(
            lambda w_q, w_lat, lat_gain, w_exp, w_out: branch(
                normed_again, w_q, w_lat, lat_gain, w_exp, w_out
            ),
            query_all,
            latent_all,
            lgain32,
            expand_all,
            output_all,
        )
        cotangents = weight_pull(stored[micro_index].astype(jnp.float32))
        totals = tuple(
            (total + piece.astype(jnp.float32) for total, piece in zip(totals, cotangents))
        )
    gain_part = jnp.where(tensor_rank == 0, gain_total, 0.0)
    grad_q, grad_lat, grad_lg, grad_e, grad_o = totals
    out_q, part_lat, part_lg, out_e, out_o, part_gain = (
        lax.psum_scatter(grad_q.astype(jnp.bfloat16), "dp", scatter_dimension=0, tiled=True).astype(
            jnp.float32
        ),
        lax.psum_scatter(
            grad_lat.astype(jnp.bfloat16), "dp", scatter_dimension=0, tiled=True
        ).astype(jnp.float32),
        lax.psum_scatter(
            grad_lg.astype(jnp.bfloat16), "dp", scatter_dimension=0, tiled=True
        ).astype(jnp.float32),
        lax.psum_scatter(grad_e.astype(jnp.bfloat16), "dp", scatter_dimension=0, tiled=True).astype(
            jnp.float32
        ),
        lax.psum_scatter(grad_o.astype(jnp.bfloat16), "dp", scatter_dimension=1, tiled=True).astype(
            jnp.float32
        ),
        lax.psum_scatter(
            gain_part.astype(jnp.bfloat16), "dp", scatter_dimension=0, tiled=True
        ).astype(jnp.float32),
    )
    out_lat, out_lg, out_gain = (
        lax.psum(part_lat.astype(jnp.bfloat16), "tensor").astype(jnp.float32),
        lax.psum(part_lg.astype(jnp.bfloat16), "tensor").astype(jnp.float32),
        lax.psum(part_gain.astype(jnp.bfloat16), "tensor").astype(jnp.float32),
    )
    return (
        results[None],
        out_gain[None],
        out_q[None],
        out_lat[None],
        out_lg[None],
        out_e[None],
        out_o[None],
    )


def solution(mesh):
    in_specs = (
        P("pipe", None, "dp", None),
        P(None, "dp", None),
        P("pipe", "dp"),
        P("pipe", "dp", "tensor"),
        P("pipe", "dp", None),
        P("pipe", "dp"),
        P("pipe", "dp", "tensor"),
        P("pipe", "tensor", "dp"),
    )
    out_specs = (
        P("pipe", None, ("dp", "tensor"), None),
        P("pipe", "dp"),
        P("pipe", "dp", "tensor"),
        P("pipe", "dp", None),
        P("pipe", "dp"),
        P("pipe", "dp", "tensor"),
        P("pipe", "tensor", "dp"),
    )
    return jax.shard_map(shards, mesh=mesh, in_specs=in_specs, out_specs=out_specs, check_vma=False)
```

profile of v0, /device:TPU:0, one launch (start us, length us, event | category | flops | bytes accessed | tf_op | source)
XLA Modules:
  0.0 381.7 jit_solution(9613141689715986463)
XLA Ops:
  7.2 1.9 copy.179
  9.3 12.9 %all_gather.19 = bf16[1,1024]{1,0:T(2,128)(2,1)S(1)} all-gather(bf16[1,256]{1,0:T(2,128)(2,1)} %param.16), channel_id=1, replica_groups=mesh['pipe'=2,'dp'=4,'tensor'=4] {'dp'}, dimensions={1}, use_global_device_ids=true | all-gather | bytes 2560 | tf_op jit(solution)/shard_map/all_gather | solution.py:71
  22.2 8.1 %all_gather.21 = bf16[1,512]{1,0:T(2,128)(2,1)S(1)} all-gather(bf16[1,128]{1,0:T(2,128)(2,1)} %param.19), channel_id=1, replica_groups=mesh['pipe'=2,'dp'=4,'tensor'=4] {'dp'}, dimensions={1}, use_global_device_ids=true | all-gather | bytes 1280 | tf_op jit(solution)/shard_map/all_gather | solution.py:74
  32.3 22.0 %all_gather.18 = bf16[1,256,1024]{2,1,0:T(8,128)(2,1)} all-gather(bf16[1,256,256]{2,1,0:T(8,128)(2,1)S(1)} %copy-done.55), channel_id=1, replica_groups=mesh['pipe'=2,'dp'=4,'tensor'=4] {'dp'}, dimensions={2}, use_global_device_ids=true | all-gather | bytes 655360 | tf_op jit(solution)/shard_map/all_gather | solution.py:76
  54.3 16.2 %all_gather.22 = bf16[1,512,512]{2,1,0:T(8,128)(2,1)S(1)} all-gather(bf16[1,128,512]{2,1,0:T(8,128)(2,1)S(1)} %copy-done.56), channel_id=1, replica_groups=mesh['pipe'=2,'dp'=4,'tensor'=4] {'dp'}, dimensions={1}, use_global_device_ids=true | all-gather | bytes 655360 | tf_op jit(solution)/shard_map/all_gather | solution.py:75
  71.3 17.4 %all_gather.23 = bf16[1,1024,384]{2,1,0:T(8,128)(2,1)} all-gather(bf16[1,256,384]{2,1,0:T(8,128)(2,1)S(1)} %copy-done.42), channel_id=1, replica_groups=mesh['pipe'=2,'dp'=4,'tensor'=4] {'dp'}, dimensions={1}, use_global_device_ids=true | all-gather | bytes 983040 | tf_op jit(solution)/shard_map/all_gather | solution.py:72
  89.5 40.7 %all-reduce.59.cloned.1.call-done = bf16[64,1024]{1,0:T(8,128)(2,1)} async-done(((bf16[64,1024]{1,0:T(8,128)(2,1)}), bf16[64,1024]{1,0:T(8,128)(2,1)}) %all-reduce.59.cloned.1.call-update) | async-done | bytes 131088 | tf_op jit(solution)/shard_map/psum | solution.py:118
  132.5 1.9 convert_multiply_fusion.16
  138.6 2.7 collective-permute-done
  142.3 28.0 %conditional.4 = (bf16[64,1024]{1,0:T(8,128)(2,1)}) conditional(s32[]{:T(128)} %convert_element_type.460, () %tuple.34, (bf16[64,1024]{1,0:T(8,128)(2,1)S(1)}, bf16[256,1024]{1,0:T(8,128)(2,1)}, f32[1024]{0:T(1024)S(1)}, f32[64,1024]{1,0:T(8,128)}, bf16[1024,576]{1,0:T(8,128)(2,1)S(1)}, /*index=5*/f32[512]{0:T(512)S(1)}, ...), branch_computations={%region_11.12_spmd, %region_12.0_spmd} | conditional | flops 367509920 | bytes 12992140 | solution.py:117
  142.3 2.0 fusion.75
  144.3 2.0 fusion.74
  155.8 1.8 fusion.56
  168.0 2.2 fusion.47
  170.8 30.4 %all-reduce.61.cloned.1.call-done = bf16[64,1024]{1,0:T(8,128)(2,1)} async-done(((bf16[64,1024]{1,0:T(8,128)(2,1)}), bf16[64,1024]{1,0:T(8,128)(2,1)}) %all-reduce.61.cloned.1.call-update) | async-done | bytes 131088 | tf_op jit(solution)/shard_map/psum | solution.py:118
  210.2 1.7 collective-permute-done.1
  236.1 9.3 %conditional.5 = (bf16[64,1024]{1,0:T(8,128)(2,1)S(1)}) conditional(s32[]{:T(128)} %convert_element_type.467, () %tuple.36, (bf16[64,1024]{1,0:T(8,128)(2,1)S(1)}, bf16[256,1024]{1,0:T(8,128)(2,1)}, f32[1024]{0:T(1024)S(1)}, f32[64,1024]{1,0:T(8,128)S(1)}, bf16[1024,576]{1,0:T(8,128)(2,1)S(1)}, /*index=5*/f32[512]{0:T(512)S(1)}, ...), branch_computations={%region_21.22_spmd, %region_22.28_spmd} | conditional | flops 367509920 | bytes 10745208 | solution.py:117
  247.8 15.5 %reduce-scatter.11.cloned.1.call-done = bf16[256,256]{1,0:T(8,128)(2,1)} async-done(((bf16[256,1024]{1,0:T(8,128)(2,1)}), bf16[256,256]{1,0:T(8,128)(2,1)}) %reduce-scatter.11.cloned.1.call-update) | async-done | bytes 131088 | tf_op jit(solution)/shard_map/reduce_scatter | solution.py:165
  264.9 28.1 %reduce-scatter.7.cloned.1.call-done = bf16[256,576]{0,1:T(8,128)(2,1)} async-done(((bf16[1024,576]{0,1:T(8,128)(2,1)}), bf16[256,576]{0,1:T(8,128)(2,1)}) %reduce-scatter.7.cloned.1.call-update) | async-done | bytes 294928 | tf_op jit(solution)/shard_map/reduce_scatter | solution.py:156
  293.1 24.0 %reduce-scatter.5.cloned.1.call-done = bf16[256,384]{1,0:T(8,128)(2,1)} async-done(((bf16[1024,384]{1,0:T(8,128)(2,1)}), bf16[256,384]{1,0:T(8,128)(2,1)}) %reduce-scatter.5.cloned.1.call-update) | async-done | bytes 196624 | tf_op jit(solution)/shard_map/reduce_scatter | solution.py:153
  318.9 33.2 %all-reduce.63.cloned.1.call-done = (bf16[64,1024]{1,0:T(8,128)(2,1)}, bf16[1,256,576]{1,2,0:T(8,128)(2,1)}) async-done(((bf16[64,1024]{1,0:T(8,128)(2,1)}, bf16[1,256,576]{1,2,0:T(8,128)(2,1)}), (bf16[64,1024]{1,0:T(8,128)(2,1)}, bf16[1,256,576]{1,2,0:T(8,128)(2,1)})) %all-reduce.63.cloned.1.call-update) | async-done | bytes 426000 | tf_op jit(solution)/shard_map/psum | solution.py:118
  353.4 11.7 %all-reduce.54 = (bf16[1024]{0:T(1024)(128)(2,1)S(1)}, bf16[512]{0:T(512)(128)(2,1)S(1)}) all-reduce(bf16[1024]{0:T(1024)(128)(2,1)S(1)} %select_convert_fusion, bf16[512]{0:T(512)(128)(2,1)S(1)} %add_convert_fusion.2), channel_id=2, replica_groups=mesh['pipe'=2,'dp'=4,'tensor'=4] {'dp'}, use_global_device_ids=true, to_apply=%region_33.34.clone | all-reduce | flops 1536 | bytes 6144
  365.2 5.9 %all-reduce.52 = (bf16[1,256]{1,0:T(2,128)(2,1)S(1)}, bf16[1,128]{1,0:T(2,128)(2,1)S(1)}) all-reduce(bf16[1,256]{1,0:T(2,128)(2,1)S(1)} %broadcast_in_dim.412, bf16[1,128]{1,0:T(2,128)(2,1)S(1)} %dynamic-slice_bitcast_fusion), channel_id=1, replica_groups=mesh['pipe'=2,'dp'=4,'tensor'=4] {'tensor'}, use_global_device_ids=true, to_apply=%region_34.35 | all-reduce | flops 384 | bytes 1536 | tf_op jit(solution)/shard_map/psum | solution.py:175
  371.6 1.8 broadcast_in_dim.440
  (459 shorter events, 80.0 us)
Async XLA Ops:
  7.2 64.1 %copy-start.2 = (bf16[1,2,64,1024]{3,2,1,0:T(8,128)(2,1)S(1)}, bf16[1,2,64,1024]{3,2,1,0:T(8,128)(2,1)}, u32[]{:S(2)}) copy-start(bf16[1,2,64,1024]{3,2,1,0:T(8,128)(2,1)} %param.14) | copy-start | bytes 786436
  7.2 81.5 %all-gather.2.cloned.1.call-start = ((), (), s32[]{:S(2)}) async-start(), calls=%async_computation.4 | async-start | bytes 1638400 | tf_op jit(solution)/shard_map/all_gather | solution.py:73
  9.2 62.2 %copy-start.42 = (bf16[1,256,384]{2,1,0:T(8,128)(2,1)S(1)}, bf16[1,256,384]{2,1,0:T(8,128)(2,1)}, u32[]{:S(2)}) copy-start(bf16[1,256,384]{2,1,0:T(8,128)(2,1)} %param.17) | copy-start | bytes 589828
  9.2 121.0 %all-reduce.59.cloned.1.call-start = ((), (), s32[]{:S(2)}) async-start(), calls=%async_computation.5 | async-start | bytes 262144 | tf_op jit(solution)/shard_map/psum | solution.py:118
  31.4 57.3 %copy-start.84 = (f32[32]{0:T(128)}, f32[32]{0:T(128)S(1)}, u32[]{:S(2)}) copy-start(f32[32]{0:T(128)S(1)} %multiply_exponential_fusion.3) | copy-start | bytes 388
  32.3 56.4 %copy-start.8 = (bf16[64,1024]{1,0:T(8,128)(2,1)}, bf16[64,1024]{1,0:T(8,128)(2,1)S(1)}, u32[]{:S(2)}) copy-start(bf16[64,1024]{1,0:T(8,128)(2,1)S(1)} %select_bitcast_fusion) | copy-start | bytes 393220
  89.5 111.8 %all-reduce.61.cloned.1.call-start = ((), (), s32[]{:S(2)}) async-start(), calls=%async_computation.6 | async-start | bytes 262144 | tf_op jit(solution)/shard_map/psum | solution.py:118
  134.3 7.0 %collective-permute-start = (bf16[64,1024]{1,0:T(8,128)(2,1)S(1)}, bf16[64,1024]{1,0:T(8,128)(2,1)}, u32[]{:S(2)}, u32[]{:S(2)}) collective-permute-start(bf16[64,1024]{1,0:T(8,128)(2,1)S(1)} %get-tuple-element.188), channel_id=1, source_target_pairs={{16,0},{17,1},{18,2},{19,3},{20,4},{21,5},{22,6},{23,7},{24,8},{25... | collective-permute-start | bytes 393224 | tf_op jit(solution)/shard_map/ppermute | solution.py:18
  170.3 75.9 %reduce-scatter.9.cloned.1.call-start = ((), (), s32[]{:S(2)}) async-start(), calls=%async_computation.9 | async-start | bytes 655360 | tf_op jit(solution)/shard_map/reduce_scatter | solution.py:162
  205.1 6.9 %collective-permute-start.1 = (bf16[64,1024]{1,0:T(8,128)(2,1)S(1)}, bf16[64,1024]{1,0:T(8,128)(2,1)S(1)}, u32[]{:S(2)}, u32[]{:S(2)}) collective-permute-start(bf16[64,1024]{1,0:T(8,128)(2,1)S(1)} %fusion.178), channel_id=1, source_target_pairs={{16,0},{17,1},{18,2},{19,3},{20,4},{21,5},{22,6},{23,7},{24,8},{25... | collective-permute-start | bytes 393224 | tf_op jit(solution)/shard_map/ppermute | solution.py:18
  219.5 43.8 %reduce-scatter.11.cloned.1.call-start = ((), (), s32[]{:S(2)}) async-start(), calls=%async_computation.10 | async-start | bytes 655360 | tf_op jit(solution)/shard_map/reduce_scatter | solution.py:165
  223.4 69.7 %reduce-scatter.7.cloned.1.call-start = ((), (), s32[]{:S(2)}) async-start(), calls=%async_computation.8 | async-start | bytes 1474560 | tf_op jit(solution)/shard_map/reduce_scatter | solution.py:156
  226.7 90.4 %reduce-scatter.5.cloned.1.call-start = ((), (), s32[]{:S(2)}) async-start(), calls=%async_computation.7 | async-start | bytes 983040 | tf_op jit(solution)/shard_map/reduce_scatter | solution.py:153
  230.6 121.5 %all-reduce.63.cloned.1.call-start = ((), (), s32[]{:S(2)}) async-start(), calls=%async_computation.11 | async-start | bytes 851968 | tf_op jit(solution)/shard_map/psum | solution.py:118
  245.4 106.7 %copy-start.97 = (f32[64]{0:T(128)S(1)}, f32[64]{0:T(128)}, u32[]{:S(2)}) copy-start(f32[64]{0:T(128)} %copy-done.95) | copy-start | bytes 772
  245.4 107.8 %copy-start.111 = (f32[64]{0:T(128)S(1)}, f32[64]{0:T(128)}, u32[]{:S(2)}) copy-start(f32[64]{0:T(128)} %copy-done.110) | copy-start | bytes 772
  245.4 107.9 %copy-start.64 = (f32[1024]{0:T(1024)S(1)}, f32[1024]{0:T(1024)}, u32[]{:S(2)}) copy-start(f32[1024]{0:T(1024)} %get-tuple-element.94) | copy-start | bytes 12292
  245.4 107.9 %copy-start.65 = (f32[1024]{0:T(1024)S(1)}, f32[1024]{0:T(1024)}, u32[]{:S(2)}) copy-start(f32[1024]{0:T(1024)} %get-tuple-element.96) | copy-start | bytes 12292
  264.9 109.0 %copy-start.112 = (f32[16]{0:T(128)S(1)}, f32[16]{0:T(128)}, u32[]{:S(2)}) copy-start(f32[16]{0:T(128)} %dynamic-slice.7) | copy-start | bytes 196
  293.1 81.0 %copy-start.57 = (bf16[16,1024]{1,0:T(8,128)(2,1)S(1)}, bf16[16,1024]{1,0:T(8,128)(2,1)}, u32[]{:S(2)}) copy-start(bf16[16,1024]{1,0:T(8,128)(2,1)} %constant_dynamic-slice_fusion) | copy-start | bytes 98308
  293.1 81.0 %copy-start.58 = (bf16[16,1024]{1,0:T(8,128)(2,1)S(1)}, bf16[16,1024]{1,0:T(8,128)(2,1)}, u32[]{:S(2)}) copy-start(bf16[16,1024]{1,0:T(8,128)(2,1)} %constant_dynamic-slice_fusion.1) | copy-start | bytes 98308
  293.1 81.0 %copy-start.92 = (pred[2]{0:T(512)(128)(4,1)S(1)}, pred[2]{0:T(512)(128)(4,1)}, u32[]{:S(2)}) copy-start(pred[2]{0:T(512)(128)(4,1)} %get-tuple-element.237) | copy-start | bytes 10
  293.1 81.0 %copy-start.94 = (pred[2]{0:T(512)(128)(4,1)S(1)}, pred[2]{0:T(512)(128)(4,1)}, u32[]{:S(2)}) copy-start(pred[2]{0:T(512)(128)(4,1)} %get-tuple-element.238) | copy-start | bytes 10
  293.1 81.0 %copy-start.105 = (pred[2]{0:T(512)(128)(4,1)S(1)}, pred[2]{0:T(512)(128)(4,1)}, u32[]{:S(2)}) copy-start(pred[2]{0:T(512)(128)(4,1)} %iota_compare_fusion.10) | copy-start | bytes 10
  (105 other events, 440.4 us)
Sparse Core Ops, SparseCore 0:
  10.1 43.6 all-gather.1
  89.6 40.6 all-reduce.58
  170.4 30.8 all-reduce.60
  219.7 21.2 reduce-scatter.8
  243.0 20.2 reduce-scatter.10
  265.5 27.5 reduce-scatter.6
  295.4 21.7 reduce-scatter.4
  319.6 32.4 all-reduce.62
where the time goes:
time: 383 us; the launch traced here: 382 us
  waiting for transfers between devices  177 us (46%)
  blocking collectives  94.1 us (25%)
  matrix products  39 us (10%)
  other arithmetic  28 us (7%)
  local copies, waits for them, and re-layouts  23.4 us (6%)
  between operations  16.9 us (4%)
    psum x3, waiting for transfers between devices, shards(): lax.psum(branch_grad.astype(jnp.bfloat16), 'tensor').astype(jnp.float32)  104 us
    reduce_scatter x1, waiting for transfers between devices, shards(): lax.psum_scatter(grad_lat.astype(jnp.bfloat16), 'dp', scatter_dimension=0...  28.1 us
    reduce_scatter x1, waiting for transfers between devices, shards(): lax.psum_scatter(grad_q.astype(jnp.bfloat16), 'dp', scatter_dimension=0,...  24 us
    all_gather x1, blocking collectives, shards(): lax.all_gather(w_output, 'dp', axis=2, tiled=True)  22 us
    all_gather x1, blocking collectives, shards(): lax.all_gather(w_query, 'dp', axis=1, tiled=True)  17.4 us
    all_gather x1, blocking collectives, shards(): lax.all_gather(expand_weight, 'dp', axis=1, tiled=True)  16.2 us
    reduce_scatter x1, waiting for transfers between devices, shards(): lax.psum_scatter(grad_o.astype(jnp.bfloat16), 'dp', scatter_dimension=1,...  15.5 us
    all_gather x1, blocking collectives, shards(): lax.all_gather(gain, 'dp', axis=1, tiled=True)  12.9 us
  transfers between devices with their start and end apart: 10, of which 8 were waited for; matrix products, arithmetic and copies ran while one was open for 10% of the time, Pallas kernels for 0%

commit v1 on v0

--- a/solution.py
+++ b/solution.py
@@ -1,6 +1,9 @@
 import jax
 import jax.numpy as jnp
 from jax import lax
+import numpy as np
+from jax.experimental import pallas as pl
+from jax.experimental.pallas import tpu as pltpu
 from jax.sharding import PartitionSpec as P
 
 NOPE = 128
@@ -185,6 +188,446 @@
     )
 
 
+MESH = pl.DeviceIdType.MESH
+BF = jnp.bfloat16
+F32 = jnp.float32
+
+
+def mm(a, b):
+    return lax.dot_general(a, b, (((1,), (0,)), ((), ())), preferred_element_type=F32)
+
+
+def mm_nt(a, b):
+    return lax.dot_general(a, b, (((1,), (1,)), ((), ())), preferred_element_type=F32)
+
+
+def mm_tn(a, b):
+    return lax.dot_general(a, b, (((0,), (0,)), ((), ())), preferred_element_type=F32)
+
+
+def half_swap(v):
+    lane = lax.broadcasted_iota(jnp.int32, v.shape, 1)
+    ahead = pltpu.roll(v, v.shape[1] - ROPE // 2, 1)
+    behind = pltpu.roll(v, ROPE // 2, 1)
+    return jnp.where(lax.rem(lane, ROPE) < ROPE // 2, ahead, behind)
+
+
+def section_kernel(
+    dims,
+    saved_ref, top_ref, small_ref, wq_ref, wl_ref, we_ref, wo_ref, cos_ref, sin_ref,
+    ig_ref, gs_ref, gq_ref, gl_ref, ge_ref, go_ref,
+    x_v, u_v, nb_v, cb_v, sm_v, wq_v, wl_v, we_v, wo_v,
+    nc_v, cc_v, mx_v, uc_v, dq_v, de_v, dl_v, part_v, rs_v, dx_v, sg_v, sr_v, st_v,
+    own_sem, line_s, line_r, pair_s, pair_r, dp_s, dp_r, ten_s, ten_r, pipe_s, pipe_r,
+):
+    n_pipe, n, n_t, micros, seq = dims
+    sec, me, ten = lax.axis_index("pipe"), lax.axis_index("dp"), lax.axis_index("tensor")
+    rows = micros * seq
+    chunk = seq // n_t
+    share = micros * chunk
+    width = x_v.shape[1]
+    wcol = wq_v.shape[1]
+    ccol = we_v.shape[1]
+    core = lax.rem(ten, 2)
+    partner = ten + 1 - 2 * core
+    half = wl_ref.shape[0] // 2
+    drains = []
+
+    def rcopy(a, b, ss, rs, dev):
+        return pltpu.make_async_remote_copy(
+            src_ref=a, dst_ref=b, send_sem=ss, recv_sem=rs, device_id=dev, device_id_type=MESH
+        )
+
+    def begin(cond, copy):
+        @pl.when(cond)
+        def _():
+            copy.start()
+
+        drains.append((cond, copy))
+
+    def dp_dev(d):
+        return (sec, d, ten)
+
+    def ten_dev(d):
+        return (sec, me, d)
+
+    barrier = pltpu.get_barrier_semaphore()
+    for j in range(n):
+        @pl.when(j != me)
+        def _():
+            pl.semaphore_signal(barrier, inc=1, device_id=dp_dev(j), device_id_type=MESH)
+
+    for j in range(n_t):
+        @pl.when(j != ten)
+        def _():
+            pl.semaphore_signal(barrier, inc=1, device_id=ten_dev(j), device_id_type=MESH)
+
+        @pl.when(sec > 0)
+        def _():
+            pl.semaphore_signal(barrier, inc=1, device_id=(sec - 1, me, j), device_id_type=MESH)
+
+        @pl.when(sec < n_pipe - 1)
+        def _():
+            pl.semaphore_signal(barrier, inc=1, device_id=(sec + 1, me, j), device_id_type=MESH)
+
+    neighbours = jnp.minimum(sec, 1) + jnp.minimum(n_pipe - 1 - sec, 1)
+    pl.semaphore_wait(barrier, n - 1 + n_t - 1 + neighbours * n_t)
+
+    def line_start(k, source, at):
+        begin(me < n - 1, rcopy(source, at(me), line_s.at[k, 0, 0], line_r.at[k, me], dp_dev(me + 1)))
+        begin(me > 0, rcopy(source, at(me), line_s.at[k, 1, 0], line_r.at[k, me], dp_dev(me - 1)))
+
+    def line_step(k, at, s, extra=None):
+        for way, block, valid, more, dest in (
+            (0, jnp.maximum(me - 1 - s, 0), me - 1 - s >= 0, me < n - 1, me + 1),
+            (1, jnp.minimum(me + 1 + s, n - 1), me + 1 + s <= n - 1, me > 0, me - 1),
+        ):
+            arrived = rcopy(at(block), at(block), line_s.at[k, way, s + 1], line_r.at[k, block], dp_dev(dest))
+
+            @pl.when(valid)
+            def _():
+                arrived.wait_recv()
+
+            if s < n - 2:
+                begin(jnp.logical_and(valid, more), arrived)
+            if extra is not None:
+                extra(block, valid, way, s)
+
+    def spread_dp(k, source, dest):
+        for j in range(n):
+            begin(j != me, rcopy(source(j), dest.at[me], dp_s.at[k, j], dp_r.at[k, me], dp_dev(j)))
+
+    def collect_dp(k, dest):
+        for j in range(n):
+            @pl.when(j != me)
+            def _():
+                rcopy(dest.at[j], dest.at[j], dp_s.at[k, j], dp_r.at[k, j], dp_dev(j)).wait_recv()
+
+    def spread_ten(k, source, dest):
+        for j in range(n_t):
+            begin(j != ten, rcopy(source(j), dest.at[ten], ten_s.at[k, j], ten_r.at[k, ten], ten_dev(j)))
+
+    def collect_ten(k, dest):
+        for j in range(n_t):
+            @pl.when(j != ten)
+            def _():
+                rcopy(dest.at[j], dest.at[j], ten_s.at[k, j], ten_r.at[k, j], ten_dev(j)).wait_recv()
+
+    wq_at = lambda b: wq_v.at[b]
+    wl_at = lambda b: wl_v.at[b, core]
+    we_at = lambda b: we_v.at[b]
+    wo_at = lambda b: wo_v.at[b]
+    dq_at = lambda b: dq_v.at[b]
+    de_at = lambda b: de_v.at[b]
+    dl_at = lambda b: dl_v.at[ten, b]
+
+    spread_dp(0, lambda j: small_ref, sm_v)
+    line_start(0, wq_ref, wq_at)
+    line_start(1, wl_ref.at[pl.ds(pl.multiple_of(core * half, half), half)], wl_at)
+    line_start(2, we_ref, we_at)
+    line_start(3, wo_ref, wo_at)
+    owns = [
+        pltpu.make_async_copy(wq_ref, wq_v.at[me], own_sem.at[0]),
+        pltpu.make_async_copy(wl_ref.at[pl.ds(0, half)], wl_v.at[me, 0], own_sem.at[1]),
+        pltpu.make_async_copy(wl_ref.at[pl.ds(half, half)], wl_v.at[me, 1], own_sem.at[2]),
+        pltpu.make_async_copy(we_ref, we_v.at[me], own_sem.at[3]),
+        pltpu.make_async_copy(wo_ref, wo_v.at[me], own_sem.at[4]),
+        pltpu.make_async_copy(small_ref, sm_v.at[me], own_sem.at[5]),
+    ]
+    for copy in owns:
+        copy.start()
+
+    for j in range(n_t):
+        for m in range(micros):
+            x_v[j * share + m * chunk : j * share + (m + 1) * chunk] = saved_ref[
+                m, j * chunk : (j + 1) * chunk
+            ]
+    for copy in owns:
+        copy.wait()
+    collect_dp(0, sm_v)
+    gain = jnp.concatenate([sm_v[d][0:1, :wcol] for d in range(n)], axis=1)
+    lgain = jnp.concatenate([sm_v[d][0:1, wcol : wcol + ccol] for d in range(n)], axis=1)
+    x32 = x_v[...].astype(F32)
+    r = lax.rsqrt(jnp.mean(x32 * x32, axis=1, keepdims=True) + EPS)
+    nb = (x32 * r * gain).astype(BF)
+    nb_v[...] = nb
+
+    pair_copies = []
+
+    def to_partner(block, valid, way, s):
+        copy = rcopy(wl_v.at[block, core], wl_v.at[block, core], pair_s.at[block], pair_r.at[block], ten_dev(partner))
+        begin(valid, copy)
+        pair_copies.append((valid, block))
+
+    for s in range(n - 1):
+        line_step(0, wq_at, s)
+        line_step(1, wl_at, s, to_partner)
+        line_step(2, we_at, s)
+        line_step(3, wo_at, s)
+    for valid, block in pair_copies:
+        @pl.when(valid)
+        def _(block=block):
+            rcopy(
+                wl_v.at[block, 1 - core], wl_v.at[block, 1 - core], pair_s.at[block], pair_r.at[block], ten_dev(partner)
+            ).wait_recv()
+
+    wq = wq_v[...].reshape(width, wq_v.shape[2])
+    wl = wl_v[...].reshape(width, wl_v.shape[3])
+    we = we_v[...].reshape(n * ccol, we_v.shape[2])
+    q = mm(nb, wq)
+    lat = mm(nb, wl)
+    rank = n * ccol
+    l32 = lat[:, :rank]
+    rl = lax.rsqrt(jnp.mean(l32 * l32, axis=1, keepdims=True) + EPS)
+    cb = (l32 * rl * lgain).astype(BF)
+    cb_v[...] = cb
+    spread_dp(1, lambda j: nb_v.at[:, pl.ds(j * wcol, wcol)], nc_v)
+    spread_dp(2, lambda j: cb_v.at[:, pl.ds(j * ccol, ccol)], cc_v)
+    ex = mm(cb, we)
+    cosine, sine = cos_ref[...], sin_ref[...]
+    lr = lat[:, rank:]
+    lr2 = jnp.concatenate([lr, lr], axis=1)
+    rk = (lr2 * cosine + half_swap(lr2) * sine).astype(BF)
+    qr_all = q[:, 2 * NOPE :]
+    qr = qr_all * cosine + half_swap(qr_all) * sine
+    lane = lax.broadcasted_iota(jnp.int32, qr.shape, 1)
+    row = lax.broadcasted_iota(jnp.int32, (rows, rows), 0)
+    col = lax.broadcasted_iota(jnp.int32, (rows, rows), 1)
+
+    def place(i):
+        return (i // share) * chunk + lax.rem(i, chunk)
+
+    same = lax.rem(row, share) // chunk == lax.rem(col, share) // chunk
+    keep = jnp.logical_and(same, place(row) >= place(col))
+    scale = (NOPE + ROPE) ** (-0.5)
+    heads = []
+    for h in range(2):
+        qn = q[:, h * NOPE : (h + 1) * NOPE].astype(BF)
+        kn = ex[:, h * (NOPE + VDIM) : h * (NOPE + VDIM) + NOPE].astype(BF)
+        vv = ex[:, h * (NOPE + VDIM) + NOPE : (h + 1) * (NOPE + VDIM)].astype(BF)
+        mask = lane < ROPE if h == 0 else lane >= ROPE
+        qh = jnp.where(mask, qr, 0.0).astype(BF)
+        scores = (mm_nt(qn, kn) + mm_nt(qh, rk)) * scale
+        scores = jnp.where(keep, scores, -1e30)
+        e = jnp.exp(scores - jnp.max(scores, axis=1, keepdims=True))
+        w32 = e / jnp.sum(e, axis=1, keepdims=True)
+        wb = w32.astype(BF)
+        mx_v[me, :, h * VDIM : (h + 1) * VDIM] = mm(wb, vv).astype(BF)
+        heads.append((qn, kn, vv, mask, qh, w32, wb))
+    spread_dp(3, lambda j: mx_v.at[me], mx_v)
+    for j in range(n):
+        @pl.when(j == me)
+        def _():
+            nc_v[j] = nb_v[:, j * wcol : (j + 1) * wcol]
+            cc_v[j] = cb_v[:, j * ccol : (j + 1) * ccol]
+
+    @pl.when(sec == n_pipe - 1)
+    def _():
+        for j in range(n_t):
+            for m in range(micros):
+                u_v[j, m * chunk : (m + 1) * chunk] = top_ref[m, j * chunk : (j + 1) * chunk]
+
+    for j in range(n_t):
+        @pl.when(sec < n_pipe - 1)
+        def _():
+            rcopy(
+                u_v.at[j], u_v.at[j], pipe_s.at[j], pipe_r.at[j], (jnp.minimum(sec + 1, n_pipe - 1), me, j)
+            ).wait_recv()
+
+    ub = u_v[...].reshape(rows, width)
+    for j in range(n):
+        uc_v[1, j] = ub[:, j * wcol : (j + 1) * wcol]
+    spread_dp(4, lambda j: uc_v.at[1, j], uc_v.at[0])
+    uc_v[0, me] = uc_v[1, me]
+    dm = jnp.zeros((rows, wo_v.shape[1]), F32)
+    for j in range(n):
+        dm = dm + mm_nt(ub[:, j * wcol : (j + 1) * wcol], wo_v[j])
+    dm = dm.astype(BF)
+    dqr = jnp.zeros((rows, 2 * ROPE), F32)
+    drk = jnp.zeros((rows, 2 * ROPE), F32)
+    for h, (qn, kn, vv, mask, qh, w32, wb) in enumerate(heads):
+        dmh = dm[:, h * VDIM : (h + 1) * VDIM]
+        dv = mm_tn(wb, dmh)
+        dw = mm_nt(dmh, vv).astype(BF).astype(F32)
+        ds = (w32 * (dw - jnp.sum(dw * w32, axis=1, keepdims=True)) * scale).astype(BF)
+        dq_v[me, :, h * NOPE : (h + 1) * NOPE] = mm(ds, kn).astype(BF)
+        dqr = dqr + jnp.where(mask, mm(ds, rk), 0.0)
+        drk = drk + mm_tn(ds, qh)
+        de_v[me, :, h * (NOPE + VDIM) : h * (NOPE + VDIM) + NOPE] = mm_tn(ds, qn).astype(BF)
+        de_v[me, :, h * (NOPE + VDIM) + NOPE : (h + 1) * (NOPE + VDIM)] = dv.astype(BF)
+    dq_v[me, :, 2 * NOPE :] = (dqr * cosine - half_swap(dqr) * sine).astype(BF)
+    drk = drk * cosine - half_swap(drk) * sine
+    drk = drk + pltpu.roll(drk, ROPE, 1)
+    line_start(4, dq_v.at[me], dq_at)
+    line_start(5, de_v.at[me], de_at)
+    dc = mm_nt(de_v[me], we)
+    dlg = jnp.sum(dc * l32 * rl, axis=0, keepdims=True)
+    dcg = dc * lgain
+    dl = rl * dcg - l32 * (rl * rl * rl) * jnp.mean(l32 * dcg, axis=1, keepdims=True)
+    dlat = jnp.concatenate([dl.astype(BF), drk[:, :ROPE].astype(BF)], axis=1)
+    dn = mm_nt(dq_v[me], wq) + mm_nt(dlat, wl)
+    part_v[:, :, :width] = dn.astype(BF).reshape(n_t, share, width)
+    part_v[:, :, width:] = dlat.reshape(n_t, share, dlat.shape[1])
+    spread_ten(0, lambda j: part_v.at[j], rs_v)
+    rs_v[ten] = part_v[ten]
+    collect_ten(0, rs_v)
+    total = jnp.sum(rs_v[...].astype(F32), axis=0)
+    dns = total[:, :width]
+    x_my = x_v[pl.ds(pl.multiple_of(ten * share, share), share)].astype(F32)
+    r_my = lax.rsqrt(jnp.mean(x_my * x_my, axis=1, keepdims=True) + EPS)
+    dng = dns * gain
+    u_my = u_v[ten].astype(F32)
+    dx = u_my + r_my * dng - x_my * (r_my * r_my * r_my) * jnp.mean(x_my * dng, axis=1, keepdims=True)
+    dx_v[...] = dx.astype(BF)
+    for j in range(n_t):
+        begin(sec > 0, rcopy(dx_v, u_v.at[ten], pipe_s.at[j], pipe_r.at[ten], (jnp.maximum(sec - 1, 0), me, j)))
+    dl_v[ten, me] = total[:, width:].astype(BF)
+    line_start(6, dl_v.at[ten, me], dl_at)
+    dgain = jnp.sum(dns * x_my * r_my, axis=0, keepdims=True)
+    for j in range(n):
+        piece = jnp.concatenate(
+            [dgain[:, j * wcol : (j + 1) * wcol], dlg[:, j * ccol : (j + 1) * ccol]], axis=1
+        )
+        sg_v[j] = jnp.broadcast_to(piece, sg_v.shape[1:])
+    spread_dp(5, lambda j: sg_v.at[j], sr_v)
+    sr_v[me] = sg_v[me]
+    for m in range(micros):
+        ig_ref[m] = dx[m * chunk : (m + 1) * chunk].astype(BF)
+    for s in range(n - 1):
+        line_step(4, dq_at, s)
+        line_step(5, de_at, s)
+        line_step(6, dl_at, s)
+    spread_ten(1, lambda j: dl_v.at[ten], dl_v)
+    collect_dp(5, sr_v)
+    st_v[ten] = jnp.sum(sr_v[...], axis=0)
+    spread_ten(2, lambda j: st_v.at[ten], st_v)
+    collect_dp(1, nc_v)
+    collect_dp(2, cc_v)
+    collect_dp(3, mx_v)
+    collect_dp(4, uc_v.at[0])
+    nc = nc_v[...].reshape(n * rows, wcol)
+    gq_ref[...] = mm_tn(nc, dq_v[...].reshape(n * rows, dq_v.shape[2]))
+    ge_ref[...] = mm_tn(cc_v[...].reshape(n * rows, ccol), de_v[...].reshape(n * rows, de_v.shape[2]))
+    go_ref[...] = mm_tn(mx_v[...].reshape(n * rows, mx_v.shape[2]), uc_v[0].reshape(n * rows, wcol))
+    collect_ten(1, dl_v)
+    acc = jnp.zeros(gl_ref.shape, F32)
+    for d in range(n):
+        block = jnp.concatenate([dl_v[j, d] for j in range(n_t)], axis=0)
+        acc = acc + mm_tn(nc_v[d], block)
+    gl_ref[...] = acc
+    collect_ten(2, st_v)
+    gs_ref[...] = jnp.sum(st_v[...], axis=0)
+    for cond, copy in drains:
+        @pl.when(cond)
+        def _(copy=copy):
+            copy.wait_send()
+
+
+def section_step(saved, top_grad, gain, w_query, w_latent, compressed_gain, expand_weight, w_output):
+    n_pipe, n, n_t = (lax.axis_size(a) for a in ("pipe", "dp", "tensor"))
+    micros, seq, width = saved.shape[1:]
+    wcol, ccol = gain.shape[1], compressed_gain.shape[1]
+    rows, share = micros * seq, micros * seq // n_t
+    qcols, lcols = w_query.shape[2], w_latent.shape[2]
+    ecols, orows = expand_weight.shape[2], w_output.shape[1]
+    small = jnp.concatenate([gain, compressed_gain], axis=1).astype(F32)
+    small = jnp.broadcast_to(small, (8, wcol + ccol))
+    per = NOPE + ROPE
+    wq = w_query[0]
+    wq = jnp.concatenate(
+        [wq[:, :NOPE], wq[:, per : per + NOPE], wq[:, NOPE:per], wq[:, per + NOPE :]], axis=1
+    )
+    order = np.arange(rows)
+    place = (order // share) * (seq // n_t) + order % (seq // n_t)
+    pair = np.arange(2 * ROPE) % (ROPE // 2)
+    angle = place[:, None] * np.exp(-np.log(10000.0) * pair / (ROPE // 2))[None, :]
+    sign = np.where(np.arange(2 * ROPE) % ROPE < ROPE // 2, -1.0, 1.0)
+    cosine = jnp.asarray(np.cos(angle), F32)
+    sine = jnp.asarray(np.sin(angle) * sign, F32)
+    vm = pl.BlockSpec(memory_space=pltpu.VMEM)
+    shape = jax.ShapeDtypeStruct
+    dma = pltpu.SemaphoreType.DMA
+    ig, gs, gq, gl, ge, go = pl.pallas_call(
+        lambda *refs: section_kernel((n_pipe, n, n_t, micros, seq), *refs),
+        name="section_step",
+        out_shape=(
+            shape((micros, seq // n_t, width), BF),
+            shape((8, wcol + ccol), F32),
+            shape((wcol, qcols), F32),
+            shape((wcol, lcols), F32),
+            shape((ccol, ecols), F32),
+            shape((orows, wcol), F32),
+        ),
+        in_specs=[vm] * 9,
+        out_specs=(vm,) * 6,
+        scratch_shapes=[
+            pltpu.VMEM((rows, width), BF),
+            pltpu.VMEM((n_t, share, width), BF),
+            pltpu.VMEM((rows, width), BF),
+            pltpu.VMEM((rows, n * ccol), BF),
+            pltpu.VMEM((n, 8, wcol + ccol), F32),
+            pltpu.VMEM((n, wcol, qcols), BF),
+            pltpu.VMEM((n, 2, wcol // 2, lcols), BF),
+            pltpu.VMEM((n, ccol, ecols), BF),
+            pltpu.VMEM((n, orows, wcol), BF),
+            pltpu.VMEM((n, rows, wcol), BF),
+            pltpu.VMEM((n, rows, ccol), BF),
+            pltpu.VMEM((n, rows, orows), BF),
+            pltpu.VMEM((2, n, rows, wcol), BF),
+            pltpu.VMEM((n, rows, qcols), BF),
+            pltpu.VMEM((n, rows, ecols), BF),
+            pltpu.VMEM((n_t, n, share, lcols), BF),
+            pltpu.VMEM((n_t, share, width + lcols), BF),
+            pltpu.VMEM((n_t, share, width + lcols), BF),
+            pltpu.VMEM((share, width), BF),
+            pltpu.VMEM((n, 8, wcol + ccol), F32),
+            pltpu.VMEM((n, 8, wcol + ccol), F32),
+            pltpu.VMEM((n_t, 8, wcol + ccol), F32),
+            dma((6,)),
+            dma((7, 2, n)),
+            dma((7, n)),
+            dma((n,)),
+            dma((n,)),
+            dma((6, n)),
+            dma((6, n)),
+            dma((3, n_t)),
+            dma((3, n_t)),
+            dma((n_t,)),
+            dma((n_t,)),
+        ],
+        compiler_params=pltpu.CompilerParams(
+            collective_id=0, has_side_effects=True, vmem_limit_bytes=60 * 1024 * 1024
+        ),
+    )(saved[0], top_grad, small, wq, w_latent[0], expand_weight[0], w_output[0], cosine, sine)
+    gq = jnp.concatenate(
+        [gq[:, :NOPE], gq[:, 2 * NOPE : 2 * NOPE + ROPE], gq[:, NOPE : 2 * NOPE], gq[:, 2 * NOPE + ROPE :]],
+        axis=1,
+    )
+    return (
+        ig[None],
+        gs[0:1, :wcol],
+        gq[None],
+        gl[None],
+        gs[0:1, wcol:],
+        ge[None],
+        go[None],
+    )
+
+
+def choose(saved, top_grad, gain, w_query, w_latent, compressed_gain, expand_weight, w_output):
+    arrays = (saved, top_grad, gain, w_query, w_latent, compressed_gain, expand_weight, w_output)
+    n_t = lax.axis_size("tensor")
+    fits = (
+        lax.axis_size("dp") > 1
+        and n_t % 2 == 0
+        and w_query.shape[2] == 2 * (NOPE + ROPE)
+        and gain.shape[1] % 128 == 0
+        and compressed_gain.shape[1] % 128 == 0
+        and saved.shape[2] % (16 * n_t) == 0
+    )
+    return section_step(*arrays) if fits else shards(*arrays)
+
+
 def solution(mesh):
     in_specs = (
         P("pipe", None, "dp", None),
@@ -205,4 +648,4 @@
         P("pipe", "dp", "tensor"),
         P("pipe", "tensor", "dp"),
     )
-    return jax.shard_map(shards, mesh=mesh, in_specs=in_specs, out_specs=out_specs, check_vma=False)
+    return jax.shard_map(choose, mesh=mesh, in_specs=in_specs, out_specs=out_specs, check_vma=False)

time: 383 us -> 119 us (0.31)
  waiting for transfers between devices: 177 us -> 0 us
  Pallas kernels: 0 us -> 105 us
  blocking collectives: 94.1 us -> 0 us
  matrix products: 39 us -> 0 us
  other arithmetic: 28 us -> 1.72 us
  between operations: 16.9 us -> 0.7 us
  local copies, waits for them, and re-layouts: 23.4 us -> 11.3 us
    pallas_call x0 -> x1, Pallas kernels: none -> 105 us  [section_step(): pl.pallas_call(lambda *refs: section_kernel((n_pipe, n, n_t, micros, seq)...]
    psum x3 -> x0, waiting for transfers between devices: 104 us -> none  [shards(): lax.psum(branch_grad.astype(jnp.bfloat16), 'tensor').astype(jnp.float32)]
    all_gather x5 -> x0, blocking collectives: 76.5 us -> none  [the longest x1 22 us: shards(): lax.all_gather(w_output, 'dp', axis=2, tiled=True)]
    reduce_scatter x4 -> x0, waiting for transfers between devices: 67.7 us -> none  [the longest x1 28.1 us: shards(): lax.psum_scatter(grad_lat.astype(jnp.bfloat16), 'dp', scatter_dimension=0...]
    dot_general x66 -> x0, matrix products: 39 us -> none  [the longest x8 9.7 us: branch(): jnp.dot(rounded, w_q, preferred_element_type=jnp.float32)]
    unnamed x1 -> x0, blocking collectives: 11.7 us -> none
    reduce_sum x16 -> x0, other arithmetic: 7.26 us -> none  [the longest x3 4.43 us: root_mean_scale(): values * lax.rsqrt(jnp.mean(values * values, axis=-1, keepdims=True) + EPS)]
    broadcast_in_dim x6 -> x1, other arithmetic: 7.85 us -> 0.92 us  [section_step(): gq[None]]
  transfers between devices with their start and end apart: 10 -> 0, of which waited for: 8 -> 0; matrix products, arithmetic and copies ran while one was open for 10% -> 0% of each run, Pallas kernels for 0% -> 0%
where the time goes in v1:
time: 119 us
  Pallas kernels  105 us (88%)
  local copies, waits for them, and re-layouts  11.3 us (9%)
  other arithmetic  1.72 us (1%)
    pallas_call x1, Pallas kernels, section_step(): pl.pallas_call(lambda *refs: section_kernel((n_pipe, n, n_t, micros, seq)...  105 us
    unnamed x23, local copies, waits for them, and re-layouts  5.91 us

profile of v1, /device:TPU:0, one launch (start us, length us, event | category | flops | bytes accessed | tf_op | source)
XLA Modules:
  0.0 118.7 jit_solution(1828334673811963383)
XLA Ops:
  0.6 0.0 copy-start.2
  0.6 1.1 fusion.2
  1.7 0.0 copy-done.2
  1.7 0.1 fusion.3
  1.8 0.0 copy-start.3
  1.8 0.8 pad_maximum_fusion.refs_3_
  2.6 0.2 copy-done.3
  2.8 0.9 copy.17
  3.7 0.7 copy-done.7
  4.4 0.7 copy-done.8
  5.0 0.6 broadcast_in_dim.20.refs_2_
  5.6 105.0 %section_step.1 = (bf16[2,16,1024]{2,1,0:T(8,128)(2,1)}, f32[8,384]{1,0:T(8,128)}, f32[256,384]{1,0:T(8,128)}, f32[256,576]{1,0:T(8,128)}, f32[128,512]{1,0:T(8,128)}, /*index=5*/f32[256,256]{1,0:T(8,128)}) custom-call(bf16[2,64,1024]{2,1,0:T(8,128)(2,1)} %bitcast.18, bf16[2,64,1024]{2,1,0:T(8,128)(2,1)} %refs_1_.1, f32[8,384]{1,0:T(8,128)} %broadcast_in_dim.20.refs_2_, ...), custom_call_target="tpu_custom_call" | custom-call | tf_op jit(solution)/shard_map/section_step/pallas_call | solution.py:550
  110.7 1.0 fusion
  111.7 0.1 copy-done
  111.8 0.1 fusion.1
  111.9 0.9 maximum_bitcast_fusion
  112.8 1.3 %slice.34 = f32[1,256]{1,0:T(1,128)} slice(f32[8,384]{1,0:T(8,128)} %get-tuple-element.14), slice={[0:1], [0:256]} | slice | bytes 2048 | tf_op jit(solution)/shard_map/slice | solution.py:608
  114.1 1.2 %slice.39 = f32[1,128]{1,0:T(1,128)} slice(f32[8,384]{1,0:T(8,128)} %get-tuple-element.14), slice={[0:1], [256:384]} | slice | bytes 1024 | tf_op jit(solution)/shard_map/slice | solution.py:611
  115.3 0.0 copy-done.1
  115.3 1.0 copy.18
  116.3 0.6 copy.22
  116.9 0.7 copy.23
  117.6 0.3 copy-done.4
  118.0 0.7 copy.24
  (11 shorter events, 0.0 us)
Async XLA Ops:
  0.6 1.1 copy-start.2
  1.8 1.0 copy-start.3
  3.7 0.7 copy-start.7
  4.4 0.7 copy-start.8
  110.7 1.1 copy-start
  111.8 3.5 %copy-start.1 = (f32[256,576]{1,0:T(8,128)S(1)}, f32[256,576]{1,0:T(8,128)}, u32[]{:S(2)}) copy-start(f32[256,576]{1,0:T(8,128)} %get-tuple-element.16) | copy-start | bytes 1769476
  115.3 1.0 copy-start.6
  115.3 1.7 %copy-start.5 = (f32[128,512]{1,0:T(8,128)S(1)}, f32[128,512]{1,0:T(8,128)}, u32[]{:S(2)}) copy-start(f32[128,512]{1,0:T(8,128)} %get-tuple-element.17) | copy-start | bytes 786436
  116.9 1.0 copy-start.4

commit v2 on v1

--- a/solution.py
+++ b/solution.py
@@ -214,11 +214,11 @@
 
 def section_kernel(
     dims,
-    saved_ref, top_ref, small_ref, wq_ref, wl_ref, we_ref, wo_ref, cos_ref, sin_ref,
-    ig_ref, gs_ref, gq_ref, gl_ref, ge_ref, go_ref,
-    x_v, u_v, nb_v, cb_v, sm_v, wq_v, wl_v, we_v, wo_v,
-    nc_v, cc_v, mx_v, uc_v, dq_v, de_v, dl_v, part_v, rs_v, dx_v, sg_v, sr_v, st_v,
-    own_sem, line_s, line_r, pair_s, pair_r, dp_s, dp_r, ten_s, ten_r, pipe_s, pipe_r,
+    saved_ref, top_ref, gain_ref, lgain_ref, wq_ref, wl_ref, we_ref, wo_ref, cos_ref, sin_ref,
+    ig_ref, gg_ref, gq_ref, gl_ref, glg_ref, ge_ref, go_ref,
+    x_v, own_v, u_v, nb_v, cb_v, sm_v, wq_v, wl_v, we_v, wo_v,
+    nc_v, cc_v, mx_v, uc_v, dq_v, de_v, dl_v, part_v, rs_v, lp_v, ls_v, q_v, lat_v, dx_v, sg_v, sr_v, st_v,
+    own_sem, line_s, line_r, pair_s, pair_r, dp_s, dp_r, ten_s, ten_r, pipe_s, pipe_r, lat_s, lat_r,
 ):
     n_pipe, n, n_t, micros, seq = dims
     sec, me, ten = lax.axis_index("pipe"), lax.axis_index("dp"), lax.axis_index("tensor")
@@ -277,11 +277,13 @@
         begin(me < n - 1, rcopy(source, at(me), line_s.at[k, 0, 0], line_r.at[k, me], dp_dev(me + 1)))
         begin(me > 0, rcopy(source, at(me), line_s.at[k, 1, 0], line_r.at[k, me], dp_dev(me - 1)))
 
-    def line_step(k, at, s, extra=None):
+    def line_step(k, at, s, extra=None, gate=None):
         for way, block, valid, more, dest in (
             (0, jnp.maximum(me - 1 - s, 0), me - 1 - s >= 0, me < n - 1, me + 1),
             (1, jnp.minimum(me + 1 + s, n - 1), me + 1 + s <= n - 1, me > 0, me - 1),
         ):
+            if gate is not None:
+                valid = jnp.logical_and(valid, gate)
             arrived = rcopy(at(block), at(block), line_s.at[k, way, s + 1], line_r.at[k, block], dp_dev(dest))
 
             @pl.when(valid)
@@ -321,7 +323,10 @@
     de_at = lambda b: de_v.at[b]
     dl_at = lambda b: dl_v.at[ten, b]
 
-    spread_dp(0, lambda j: small_ref, sm_v)
+    own_v[:, :wcol] = jnp.broadcast_to(gain_ref[...].astype(F32), (8, wcol))
+    own_v[:, wcol:] = jnp.broadcast_to(lgain_ref[...].astype(F32), (8, ccol))
+    spread_dp(0, lambda j: own_v, sm_v)
+    sm_v[me] = own_v[...]
     line_start(0, wq_ref, wq_at)
     line_start(1, wl_ref.at[pl.ds(pl.multiple_of(core * half, half), half)], wl_at)
     line_start(2, we_ref, we_at)
@@ -332,7 +337,6 @@
         pltpu.make_async_copy(wl_ref.at[pl.ds(half, half)], wl_v.at[me, 1], own_sem.at[2]),
         pltpu.make_async_copy(we_ref, we_v.at[me], own_sem.at[3]),
         pltpu.make_async_copy(wo_ref, wo_v.at[me], own_sem.at[4]),
-        pltpu.make_async_copy(small_ref, sm_v.at[me], own_sem.at[5]),
     ]
     for copy in owns:
         copy.start()
@@ -359,23 +363,52 @@
         begin(valid, copy)
         pair_copies.append((valid, block))
 
+    def cols(b):
+        return pl.ds(pl.multiple_of(b * wcol, wcol), wcol)
+
+    def use_query(b):
+        q_v[...] += mm(nb_v[:, cols(b)], wq_v[b])
+
+    def use_latent(b):
+        lat_v[...] += mm_nt(nb_v[:, cols(b)], wl_v[b].reshape(2 * half, wcol))
+
+    last = sec == n_pipe - 1
+
+    @pl.when(last)
+    def _():
+        for j in range(n_t):
+            for m in range(micros):
+                u_v[j, m * chunk : (m + 1) * chunk] = top_ref[m, j * chunk : (j + 1) * chunk]
+
+    q_v[...] = mm(nb_v[:, cols(me)], wq_v[me])
+    lat_v[...] = mm_nt(nb_v[:, cols(me)], wl_v[me].reshape(2 * half, wcol))
+
+    def settle_latent(pairs):
+        for valid, block in pairs:
+            @pl.when(valid)
+            def _(block=block):
+                rcopy(
+                    wl_v.at[block, 1 - core], wl_v.at[block, 1 - core], pair_s.at[block], pair_r.at[block], ten_dev(partner)
+                ).wait_recv()
+                use_latent(block)
+
     for s in range(n - 1):
         line_step(0, wq_at, s)
         line_step(1, wl_at, s, to_partner)
+        for valid, block in pair_copies[-2:]:
+            @pl.when(valid)
+            def _(block=block):
+                use_query(block)
+
         line_step(2, we_at, s)
         line_step(3, wo_at, s)
-    for valid, block in pair_copies:
-        @pl.when(valid)
-        def _(block=block):
-            rcopy(
-                wl_v.at[block, 1 - core], wl_v.at[block, 1 - core], pair_s.at[block], pair_r.at[block], ten_dev(partner)
-            ).wait_recv()
+        settle_latent(pair_copies[-2:])
 
     wq = wq_v[...].reshape(width, wq_v.shape[2])
-    wl = wl_v[...].reshape(width, wl_v.shape[3])
+    wl = [wl_v[d].reshape(2 * half, wcol) for d in range(n)]
     we = we_v[...].reshape(n * ccol, we_v.shape[2])
-    q = mm(nb, wq)
-    lat = mm(nb, wl)
+    q = q_v[...]
+    lat = lat_v[...]
     rank = n * ccol
     l32 = lat[:, :rank]
     rl = lax.rsqrt(jnp.mean(l32 * l32, axis=1, keepdims=True) + EPS)
@@ -388,9 +421,12 @@
     lr = lat[:, rank:]
     lr2 = jnp.concatenate([lr, lr], axis=1)
     rk = (lr2 * cosine + half_swap(lr2) * sine).astype(BF)
-    qr_all = q[:, 2 * NOPE :]
+    lane = lax.broadcasted_iota(jnp.int32, (rows, 2 * ROPE), 1)
+    low = lane < ROPE
+    q1, q2 = q[:, NOPE : 2 * NOPE], q[:, 2 * NOPE :]
+    nope = (q[:, :NOPE], pltpu.roll(jnp.where(low, q2, q1), ROPE, 1))
+    qr_all = jnp.where(low, q1, q2)
     qr = qr_all * cosine + half_swap(qr_all) * sine
-    lane = lax.broadcasted_iota(jnp.int32, qr.shape, 1)
     row = lax.broadcasted_iota(jnp.int32, (rows, rows), 0)
     col = lax.broadcasted_iota(jnp.int32, (rows, rows), 1)
 
@@ -402,10 +438,10 @@
     scale = (NOPE + ROPE) ** (-0.5)
     heads = []
     for h in range(2):
-        qn = q[:, h * NOPE : (h + 1) * NOPE].astype(BF)
+        qn = nope[h].astype(BF)
         kn = ex[:, h * (NOPE + VDIM) : h * (NOPE + VDIM) + NOPE].astype(BF)
         vv = ex[:, h * (NOPE + VDIM) + NOPE : (h + 1) * (NOPE + VDIM)].astype(BF)
-        mask = lane < ROPE if h == 0 else lane >= ROPE
+        mask = low if h == 0 else jnp.logical_not(low)
         qh = jnp.where(mask, qr, 0.0).astype(BF)
         scores = (mm_nt(qn, kn) + mm_nt(qh, rk)) * scale
         scores = jnp.where(keep, scores, -1e30)
@@ -421,12 +457,6 @@
             nc_v[j] = nb_v[:, j * wcol : (j + 1) * wcol]
             cc_v[j] = cb_v[:, j * ccol : (j + 1) * ccol]
 
-    @pl.when(sec == n_pipe - 1)
-    def _():
-        for j in range(n_t):
-            for m in range(micros):
-                u_v[j, m * chunk : (m + 1) * chunk] = top_ref[m, j * chunk : (j + 1) * chunk]
-
     for j in range(n_t):
         @pl.when(sec < n_pipe - 1)
         def _():
@@ -445,17 +475,22 @@
     dm = dm.astype(BF)
     dqr = jnp.zeros((rows, 2 * ROPE), F32)
     drk = jnp.zeros((rows, 2 * ROPE), F32)
+    dqn = []
     for h, (qn, kn, vv, mask, qh, w32, wb) in enumerate(heads):
         dmh = dm[:, h * VDIM : (h + 1) * VDIM]
         dv = mm_tn(wb, dmh)
         dw = mm_nt(dmh, vv).astype(BF).astype(F32)
         ds = (w32 * (dw - jnp.sum(dw * w32, axis=1, keepdims=True)) * scale).astype(BF)
-        dq_v[me, :, h * NOPE : (h + 1) * NOPE] = mm(ds, kn).astype(BF)
+        dqn.append(mm(ds, kn))
         dqr = dqr + jnp.where(mask, mm(ds, rk), 0.0)
         drk = drk + mm_tn(ds, qh)
         de_v[me, :, h * (NOPE + VDIM) : h * (NOPE + VDIM) + NOPE] = mm_tn(ds, qn).astype(BF)
         de_v[me, :, h * (NOPE + VDIM) + NOPE : (h + 1) * (NOPE + VDIM)] = dv.astype(BF)
-    dq_v[me, :, 2 * NOPE :] = (dqr * cosine - half_swap(dqr) * sine).astype(BF)
+    dqr = dqr * cosine - half_swap(dqr) * sine
+    turned = pltpu.roll(dqn[1], ROPE, 1)
+    dq_v[me, :, :NOPE] = dqn[0].astype(BF)
+    dq_v[me, :, NOPE : 2 * NOPE] = jnp.where(low, dqr, turned).astype(BF)
+    dq_v[me, :, 2 * NOPE :] = jnp.where(low, turned, dqr).astype(BF)
     drk = drk * cosine - half_swap(drk) * sine
     drk = drk + pltpu.roll(drk, ROPE, 1)
     line_start(4, dq_v.at[me], dq_at)
@@ -465,14 +500,18 @@
     dcg = dc * lgain
     dl = rl * dcg - l32 * (rl * rl * rl) * jnp.mean(l32 * dcg, axis=1, keepdims=True)
     dlat = jnp.concatenate([dl.astype(BF), drk[:, :ROPE].astype(BF)], axis=1)
-    dn = mm_nt(dq_v[me], wq) + mm_nt(dlat, wl)
-    part_v[:, :, :width] = dn.astype(BF).reshape(n_t, share, width)
-    part_v[:, :, width:] = dlat.reshape(n_t, share, dlat.shape[1])
+    dn = mm_nt(dq_v[me], wq) + jnp.concatenate([mm(dlat, wl[d]) for d in range(n)], axis=1)
+    part_v[...] = dn.astype(BF).reshape(n_t, share, width)
     spread_ten(0, lambda j: part_v.at[j], rs_v)
+    lp_v[...] = dlat.reshape(n_t, share, dlat.shape[1])
+    spread_ten(3, lambda j: lp_v.at[j], ls_v)
     rs_v[ten] = part_v[ten]
+    ls_v[ten] = lp_v[ten]
+    bottom = sec == 0
+    line_step(4, dq_at, 0, gate=bottom)
+    line_step(5, de_at, 0, gate=bottom)
     collect_ten(0, rs_v)
-    total = jnp.sum(rs_v[...].astype(F32), axis=0)
-    dns = total[:, :width]
+    dns = jnp.sum(rs_v[...].astype(F32), axis=0)
     x_my = x_v[pl.ds(pl.multiple_of(ten * share, share), share)].astype(F32)
     r_my = lax.rsqrt(jnp.mean(x_my * x_my, axis=1, keepdims=True) + EPS)
     dng = dns * gain
@@ -481,7 +520,8 @@
     dx_v[...] = dx.astype(BF)
     for j in range(n_t):
         begin(sec > 0, rcopy(dx_v, u_v.at[ten], pipe_s.at[j], pipe_r.at[ten], (jnp.maximum(sec - 1, 0), me, j)))
-    dl_v[ten, me] = total[:, width:].astype(BF)
+    collect_ten(3, ls_v)
+    dl_v[ten, me] = jnp.sum(ls_v[...].astype(F32), axis=0).astype(BF)
     line_start(6, dl_v.at[ten, me], dl_at)
     dgain = jnp.sum(dns * x_my * r_my, axis=0, keepdims=True)
     for j in range(n):
@@ -491,13 +531,25 @@
         sg_v[j] = jnp.broadcast_to(piece, sg_v.shape[1:])
     spread_dp(5, lambda j: sg_v.at[j], sr_v)
     sr_v[me] = sg_v[me]
+
+    def to_tensor(block, valid=None, way=0, s=0):
+        for j in range(n_t):
+            cond = j != ten if valid is None else jnp.logical_and(valid, j != ten)
+            begin(
+                cond,
+                rcopy(dl_v.at[ten, block], dl_v.at[ten, block], lat_s.at[j, block], lat_r.at[ten, block], ten_dev(j)),
+            )
+
+    to_tensor(me)
+    line_step(4, dq_at, 0, gate=sec > 0)
+    line_step(5, de_at, 0, gate=sec > 0)
     for m in range(micros):
         ig_ref[m] = dx[m * chunk : (m + 1) * chunk].astype(BF)
-    for s in range(n - 1):
+    for s in range(1, n - 1):
+        line_step(6, dl_at, s - 1, to_tensor)
         line_step(4, dq_at, s)
         line_step(5, de_at, s)
-        line_step(6, dl_at, s)
-    spread_ten(1, lambda j: dl_v.at[ten], dl_v)
+    line_step(6, dl_at, n - 2, to_tensor)
     collect_dp(5, sr_v)
     st_v[ten] = jnp.sum(sr_v[...], axis=0)
     spread_ten(2, lambda j: st_v.at[ten], st_v)
@@ -509,14 +561,21 @@
     gq_ref[...] = mm_tn(nc, dq_v[...].reshape(n * rows, dq_v.shape[2]))
     ge_ref[...] = mm_tn(cc_v[...].reshape(n * rows, ccol), de_v[...].reshape(n * rows, de_v.shape[2]))
     go_ref[...] = mm_tn(mx_v[...].reshape(n * rows, mx_v.shape[2]), uc_v[0].reshape(n * rows, wcol))
-    collect_ten(1, dl_v)
+    for j in range(n_t):
+        for d in range(n):
+            @pl.when(j != ten)
+            def _():
+                rcopy(dl_v.at[j, d], dl_v.at[j, d], lat_s.at[j, d], lat_r.at[j, d], ten_dev(j)).wait_recv()
+
     acc = jnp.zeros(gl_ref.shape, F32)
     for d in range(n):
         block = jnp.concatenate([dl_v[j, d] for j in range(n_t)], axis=0)
-        acc = acc + mm_tn(nc_v[d], block)
+        acc = acc + mm_tn(block, nc_v[d])
     gl_ref[...] = acc
     collect_ten(2, st_v)
-    gs_ref[...] = jnp.sum(st_v[...], axis=0)
+    summed = jnp.sum(st_v[...], axis=0)
+    gg_ref[...] = summed[0:1, :wcol]
+    glg_ref[...] = summed[0:1, wcol:]
     for cond, copy in drains:
         @pl.when(cond)
         def _(copy=copy):
@@ -530,13 +589,6 @@
     rows, share = micros * seq, micros * seq // n_t
     qcols, lcols = w_query.shape[2], w_latent.shape[2]
     ecols, orows = expand_weight.shape[2], w_output.shape[1]
-    small = jnp.concatenate([gain, compressed_gain], axis=1).astype(F32)
-    small = jnp.broadcast_to(small, (8, wcol + ccol))
-    per = NOPE + ROPE
-    wq = w_query[0]
-    wq = jnp.concatenate(
-        [wq[:, :NOPE], wq[:, per : per + NOPE], wq[:, NOPE:per], wq[:, per + NOPE :]], axis=1
-    )
     order = np.arange(rows)
     place = (order // share) * (seq // n_t) + order % (seq // n_t)
     pair = np.arange(2 * ROPE) % (ROPE // 2)
@@ -547,27 +599,29 @@
     vm = pl.BlockSpec(memory_space=pltpu.VMEM)
     shape = jax.ShapeDtypeStruct
     dma = pltpu.SemaphoreType.DMA
-    ig, gs, gq, gl, ge, go = pl.pallas_call(
+    ig, gg, gq, gl, glg, ge, go = pl.pallas_call(
         lambda *refs: section_kernel((n_pipe, n, n_t, micros, seq), *refs),
         name="section_step",
         out_shape=(
             shape((micros, seq // n_t, width), BF),
-            shape((8, wcol + ccol), F32),
+            shape((1, wcol), F32),
             shape((wcol, qcols), F32),
-            shape((wcol, lcols), F32),
+            shape((lcols, wcol), F32),
+            shape((1, ccol), F32),
             shape((ccol, ecols), F32),
             shape((orows, wcol), F32),
         ),
-        in_specs=[vm] * 9,
-        out_specs=(vm,) * 6,
+        in_specs=[vm] * 10,
+        out_specs=(vm,) * 7,
         scratch_shapes=[
             pltpu.VMEM((rows, width), BF),
+            pltpu.VMEM((8, wcol + ccol), F32),
             pltpu.VMEM((n_t, share, width), BF),
             pltpu.VMEM((rows, width), BF),
             pltpu.VMEM((rows, n * ccol), BF),
             pltpu.VMEM((n, 8, wcol + ccol), F32),
             pltpu.VMEM((n, wcol, qcols), BF),
-            pltpu.VMEM((n, 2, wcol // 2, lcols), BF),
+            pltpu.VMEM((n, 2, lcols // 2, wcol), BF),
             pltpu.VMEM((n, ccol, ecols), BF),
             pltpu.VMEM((n, orows, wcol), BF),
             pltpu.VMEM((n, rows, wcol), BF),
@@ -577,8 +631,12 @@
             pltpu.VMEM((n, rows, qcols), BF),
             pltpu.VMEM((n, rows, ecols), BF),
             pltpu.VMEM((n_t, n, share, lcols), BF),
-            pltpu.VMEM((n_t, share, width + lcols), BF),
-            pltpu.VMEM((n_t, share, width + lcols), BF),
+            pltpu.VMEM((n_t, share, width), BF),
+            pltpu.VMEM((n_t, share, width), BF),
+            pltpu.VMEM((n_t, share, lcols), BF),
+            pltpu.VMEM((n_t, share, lcols), BF),
+            pltpu.VMEM((rows, qcols), F32),
+            pltpu.VMEM((rows, lcols), F32),
             pltpu.VMEM((share, width), BF),
             pltpu.VMEM((n, 8, wcol + ccol), F32),
             pltpu.VMEM((n, 8, wcol + ccol), F32),
@@ -590,28 +648,21 @@
             dma((n,)),
             dma((6, n)),
             dma((6, n)),
-            dma((3, n_t)),
-            dma((3, n_t)),
+            dma((4, n_t)),
+            dma((4, n_t)),
             dma((n_t,)),
             dma((n_t,)),
+            dma((n_t, n)),
+            dma((n_t, n)),
         ],
         compiler_params=pltpu.CompilerParams(
             collective_id=0, has_side_effects=True, vmem_limit_bytes=60 * 1024 * 1024
         ),
-    )(saved[0], top_grad, small, wq, w_latent[0], expand_weight[0], w_output[0], cosine, sine)
-    gq = jnp.concatenate(
-        [gq[:, :NOPE], gq[:, 2 * NOPE : 2 * NOPE + ROPE], gq[:, NOPE : 2 * NOPE], gq[:, 2 * NOPE + ROPE :]],
-        axis=1,
-    )
-    return (
-        ig[None],
-        gs[0:1, :wcol],
-        gq[None],
-        gl[None],
-        gs[0:1, wcol:],
-        ge[None],
-        go[None],
-    )
+    )(
+        saved[0], top_grad, gain, compressed_gain, w_query[0], w_latent[0].T,
+        expand_weight[0], w_output[0], cosine, sine,
+    )
+    return ig[None], gg, gq[None], gl.T[None], glg, ge[None], go[None]
 
 
 def choose(saved, top_grad, gain, w_query, w_latent, compressed_gain, expand_weight, w_output):

time: 119 us -> 109 us (0.916)
  Pallas kernels: 105 us -> 101 us
  local copies, waits for them, and re-layouts: 11.3 us -> 7.63 us
  other arithmetic: 1.72 us -> 0 us
    slice x6 -> x0, local copies, waits for them, and re-layouts: 4.73 us -> none  [the longest x1 1.26 us: section_step(): gs[0:1, :wcol]]
    pallas_call x1, Pallas kernels: 105 us -> 101 us  [section_step(): pl.pallas_call(lambda *refs: section_kernel((n_pipe, n, n_t, micros, seq)...]
    unnamed x23 -> x15, local copies, waits for them, and re-layouts: 5.91 us -> 7.63 us
where the time goes in v2:
time: 109 us
  Pallas kernels  101 us (93%)
  local copies, waits for them, and re-layouts  7.63 us (7%)
    pallas_call x1, Pallas kernels, section_step(): pl.pallas_call(lambda *refs: section_kernel((n_pipe, n, n_t, micros, seq)...  101 us
    unnamed x15, local copies, waits for them, and re-layouts  7.63 us

profile of v2, /device:TPU:0, one launch (start us, length us, event | category | flops | bytes accessed | tf_op | source)
XLA Modules:
  0.0 108.8 jit_solution(2957184806142628833)
XLA Ops:
  0.6 100.6 %section_step.1 = (bf16[2,16,1024]{2,1,0:T(8,128)(2,1)}, f32[1,256]{1,0:T(1,128)}, f32[256,384]{1,0:T(8,128)}, f32[576,256]{1,0:T(8,128)}, f32[1,128]{1,0:T(1,12...) custom-call(bf16[2,64,1024]{2,1,0:T(8,128)(2,1)} %bitcast.19, bf16[2,64,1024]{2,1,0:T(8,128)(2,1)} %refs_1_.1, ...), custom_call_target="tpu_custom_call" | custom-call | tf_op jit(solution)/shard_map/section_step/pallas_call | solution.py:602
  101.2 0.0 copy-start
  101.2 1.5 %copy.24 = bf16[1,2,16,1024]{3,2,1,0:T(8,128)(2,1)} copy(bf16[1,2,16,1024]{3,2,1,0:T(8,128)(2,1)} %bitcast.23) | data formatting | bytes 131072
  102.7 1.2 %copy.25 = f32[1,256]{1,0:T(1,128)} copy(f32[1,256]{1,0:T(1,128)} %get-tuple-element.29) | data formatting | bytes 2048
  104.0 1.8 %copy.26 = f32[1,256,384]{2,1,0:T(8,128)} copy(f32[1,256,384]{2,1,0:T(8,128)} %bitcast.15) | data formatting | bytes 786432
  105.8 0.0 copy-done
  105.8 0.0 copy-start.3
  105.8 0.0 copy-start.2
  105.8 0.8 copy.27
  106.6 0.0 copy-done.3
  106.6 0.5 copy.28
  107.1 0.0 copy-done.2
  107.1 0.0 copy-start.1
  107.1 0.7 copy.29
  107.8 0.3 copy-done.1
  108.1 0.7 copy.30
Async XLA Ops:
  101.2 4.6 %copy-start = (f32[576,256]{1,0:T(8,128)S(1)}, f32[576,256]{1,0:T(8,128)}, u32[]{:S(2)}) copy-start(f32[576,256]{1,0:T(8,128)} %get-tuple-element.17) | copy-start | bytes 1769476
  105.8 0.8 copy-start.3
  105.8 1.3 %copy-start.2 = (f32[128,512]{1,0:T(8,128)S(1)}, f32[128,512]{1,0:T(8,128)}, u32[]{:S(2)}) copy-start(f32[128,512]{1,0:T(8,128)} %get-tuple-element.19) | copy-start | bytes 786436
  107.1 1.0 copy-start.1

commit v3 on v2

--- a/solution.py
+++ b/solution.py
@@ -580,6 +580,11 @@
         @pl.when(cond)
         def _(copy=copy):
             copy.wait_send()
+
+
+def hand_over(*refs):
+    for source, dest in zip(refs[:7], refs[7:]):
+        dest[...] = source[...]
 
 
 def section_step(saved, top_grad, gain, w_query, w_latent, compressed_gain, expand_weight, w_output):
@@ -662,6 +667,14 @@
         saved[0], top_grad, gain, compressed_gain, w_query[0], w_latent[0].T,
         expand_weight[0], w_output[0], cosine, sine,
     )
+    parts = (ig, gg, gq, gl, glg, ge, go)
+    ig, gg, gq, gl, glg, ge, go = pl.pallas_call(
+        hand_over,
+        name="hand_over",
+        out_shape=tuple(shape(p.shape, p.dtype) for p in parts),
+        in_specs=[vm] * 7,
+        out_specs=(vm,) * 7,
+    )(*parts)
     return ig[None], gg, gq[None], gl.T[None], glg, ge[None], go[None]
 
 

time: 109 us -> 104 us (0.954)
  local copies, waits for them, and re-layouts: 7.63 us -> 0 us
  Pallas kernels: 101 us -> 103 us
    unnamed x15 -> x0, local copies, waits for them, and re-layouts: 7.63 us -> none
    pallas_call x0 -> x1, Pallas kernels: none -> 2.54 us  [section_step(): pl.pallas_call(hand_over, name='hand_over', out_shape=tuple((shape(p.shap...]
where the time goes in v3:
time: 104 us
  Pallas kernels  103 us (99%)
    pallas_call x1, Pallas kernels, section_step(): pl.pallas_call(lambda *refs: section_kernel((n_pipe, n, n_t, micros, seq)...  101 us
    pallas_call x1, Pallas kernels, section_step(): pl.pallas_call(hand_over, name='hand_over', out_shape=tuple((shape(p.shap...  2.54 us

profile of v3, /device:TPU:0, one launch (start us, length us, event | category | flops | bytes accessed | tf_op | source)
XLA Modules:
  0.0 103.7 jit_solution(9494235014352837012)
XLA Ops:
  0.6 100.6 %section_step.1 = (bf16[2,16,1024]{2,1,0:T(8,128)(2,1)}, f32[1,256]{1,0:T(1,128)}, f32[256,384]{1,0:T(8,128)}, f32[576,256]{1,0:T(8,128)}, f32[1,128]{1,0:T(1,12...) custom-call(bf16[2,64,1024]{2,1,0:T(8,128)(2,1)} %bitcast.15, bf16[2,64,1024]{2,1,0:T(8,128)(2,1)} %refs_1_.1, ...), custom_call_target="tpu_custom_call" | custom-call | tf_op jit(solution)/shard_map/section_step/pallas_call | solution.py:607
  101.2 2.5 %hand_over.1 = (bf16[2,16,1024]{2,1,0:T(8,128)(2,1)}, f32[1,256]{1,0:T(1,128)}, f32[256,384]{1,0:T(8,128)}, f32[576,256]{1,0:T(8,128)}, f32[1,128]{1,0:T(1,128)}...) custom-call(bf16[2,16,1024]{2,1,0:T(8,128)(2,1)} %get-tuple-element.21.refs_0_, f32[1,256]{1,0:T(1,128)} %get-tuple-element.22.refs_1_, ...), custom_call_target="tpu_custom_call" | custom-call | tf_op jit(solution)/shard_map/hand_over/pallas_call | solution.py:671
